TPU v7x, 32 devices: a whole 2x2x4 slice. The times are simulated.
32 devices in a mesh: fsdp: 8 (over y, x, core), seq: 4 (over z).
Axes of the slice: x: 2, y: 2, z: 4, core: 2. Of those that a mesh axis runs over, the one named last changes fastest.
Arguments:
- layer_input: bfloat16 [8, 512, 4096], P('fsdp', 'seq'), may hold values from -6 to 6
- dt_weight: bfloat16 [4096, 64], P('fsdp'), may hold values from -0.09375 to 0.09375
- dt_bias: float32 [64], replicated, may hold values from -2 to -0.5
- decay_rate: float32 [64], replicated, may hold values from 0.0005 to 0.25
- ssm_input: bfloat16 [8, 512, 2048], P('fsdp', 'seq'), may hold values from -6 to 6
- in_basis: bfloat16 [8, 512, 512], P('fsdp', 'seq'), may hold values from -0.59765625 to 0.59765625
- out_basis: bfloat16 [8, 512, 512], P('fsdp', 'seq'), may hold values from -0.59765625 to 0.59765625
- out_cotangent: bfloat16 [8, 512, 2048], P('fsdp', 'seq'), may hold values from -6 to 6
Outputs:
- grad_input: bfloat16 [8, 512, 2048], P('fsdp', 'seq')
- grad_in_basis: bfloat16 [8, 512, 512], P('fsdp', 'seq')
- grad_out_basis: bfloat16 [8, 512, 512], P('fsdp', 'seq')
- grad_dt_weight: float32 [4096, 64], P('fsdp')
All inputs are finite; a program needn't handle non-finite values.
Results may differ from a plain program's by a relative error of at most 0.011.
Values may be sent and summed in bfloat16 or wider, within the bound.
A program may use at most 64 MiB of HBM per device.

v0:
```python
import jax
import jax.numpy as jnp
from jax import lax
from jax.sharding import PartitionSpec as P

STATE = 128
HIGH = lax.Precision.HIGHEST


def entering(value, axis, combine, identity):
    devices, position = (lax.axis_size(axis), lax.axis_index(axis))
    everything = jax.tree.map(
        lambda part, kind: lax.all_gather(part.astype(kind), axis),
        value,
        (jnp.bfloat16, jnp.bfloat16),
    )
    start = jax.tree.map(
        lambda part, zero: jnp.broadcast_to(jnp.asarray(zero, part.dtype), part.shape),
        value,
        identity,
    )

    def entering_step(k, before):
        reached = k < position
        new = combine(
            before, jax.tree.map(lambda part, own: part[k].astype(own.dtype), everything, value)
        )
        return jax.tree.map(lambda a, b: jnp.where(reached, a, b), new, before)

    return lax.fori_loop(0, devices, entering_step, start)


def prefix(value, axis, join, neutral):
    count, mine = (lax.axis_size(axis), lax.axis_index(axis))
    pieces = jax.tree.map(lambda part: lax.all_gather(part, axis), value)
    pieces = jax.tree.map(lambda part: part[::-1], pieces)
    mine = count - 1 - mine
    subtotal = jax.tree.map(
        lambda part, zero: jnp.full_like(part, 0) + jnp.asarray(zero, part.dtype), value, neutral
    )

    def prefix_step(position, subtotal):
        longer = join(subtotal, jax.tree.map(lambda part: part[position], pieces))
        return jax.tree.map(lambda new, old: jnp.where(position < mine, new, old), longer, subtotal)

    return lax.fori_loop(0, count - 1, prefix_step, subtotal)


def compose(earlier, later):
    decay_e, value_e = earlier
    decay_l, value_l = later
    return (decay_l * decay_e, value_l + decay_l[:, None, None] * value_e)


def body(
    layer_input, dt_weight, dt_bias, decay_rate, ssm_input, in_basis, out_basis, out_cotangent
):
    tokens = layer_input[0]
    length = tokens.shape[0]
    heads = dt_weight.shape[1]
    groups = in_basis.shape[2] // STATE
    per_group = heads // groups
    head_size = ssm_input.shape[2] // heads
    columns = tokens
    raw = (
        jnp.dot(
            columns,
            lax.all_gather(dt_weight, "fsdp", axis=0, tiled=True),
            preferred_element_type=jnp.float32,
        )
        + dt_bias
    )
    step_size = jax.nn.softplus(raw)
    rate_grid = decay_rate.reshape(groups, per_group)
    step_grid = step_size.reshape(length, groups, per_group)
    cumulative = jnp.cumsum(-decay_rate * step_size, axis=0).reshape(length, groups, per_group)
    final = cumulative[-1]
    tail = jnp.exp(final[None] - cumulative)
    leading = jnp.exp(cumulative)
    inputs_half = ssm_input[0].reshape(length, groups, per_group, head_size)
    upstream_half = out_cotangent[0].reshape(length, groups, per_group, head_size)
    bin_half = in_basis[0].reshape(length, groups, STATE)
    bout_half = out_basis[0].reshape(length, groups, STATE)
    inputs = inputs_half.astype(jnp.float32)
    upstream = upstream_half.astype(jnp.float32)
    basis_in = bin_half.astype(jnp.float32)
    basis_out = bout_half.astype(jnp.float32)
    position = jnp.arange(length)
    lower = position[:, None] >= position[None, :]
    cum_rows = cumulative.transpose(1, 2, 0)
    spread = cum_rows[:, :, :, None] - cum_rows[:, :, None, :]
    decay_mat = jnp.where(lower, jnp.exp(jnp.where(lower, spread, 0.0)), 0.0)
    intersection = jnp.einsum(
        "tgn,sgn->gts", bout_half, bin_half, preferred_element_type=jnp.float32
    )
    weighted = decay_mat * intersection[:, None]
    step_cols = step_grid.transpose(1, 2, 0)[:, :, None, :]
    local_state = jnp.einsum(
        "sgk,sgkp,sgn->gkpn", tail * step_grid, inputs, basis_in, precision=HIGH
    )
    local_grad = jnp.einsum("tgk,tgkp,tgn->gkpn", leading, upstream, basis_out, precision=HIGH)
    block_decay = jnp.exp(final).reshape(heads)
    flat_shape = (heads, head_size, STATE)
    grid_shape = (groups, per_group, head_size, STATE)
    identity = (jnp.ones((heads,), jnp.float32), jnp.zeros(flat_shape, jnp.float32))
    entry = entering((block_decay, local_state.reshape(flat_shape)), "seq", compose, identity)[
        1
    ].reshape(grid_shape)
    later = prefix((block_decay, local_grad.reshape(flat_shape)), "seq", compose, identity)[
        1
    ].reshape(grid_shape)
    pair = jnp.einsum(
        "tgkp,sgkp->gkts", upstream_half, inputs_half, preferred_element_type=jnp.float32
    )
    through = jnp.einsum("gkts,tgkp->sgkp", weighted, upstream, precision=HIGH)
    carried = jnp.einsum("sgn,gkpn->sgkp", basis_in, later, precision=HIGH)
    inner_x = through + tail[..., None] * carried
    grad_x = step_grid[..., None] * inner_x
    direct = jnp.sum(inputs * inner_x, axis=-1)
    scaled = decay_mat * pair * step_cols
    joint = jnp.sum(scaled, axis=1)
    moment = scaled * intersection[:, None]
    change = (jnp.sum(moment, axis=-1) - jnp.sum(moment, axis=-2)).transpose(2, 0, 1)
    grad_b = jnp.einsum("gts,tgn->sgn", joint, basis_out, precision=HIGH)
    grad_b = grad_b + jnp.einsum(
        "sgk,sgkp,gkpn->sgn", step_grid * tail, inputs, later, precision=HIGH
    )
    state_read = jnp.einsum("tgkp,gkpn->tgkn", upstream, entry, precision=HIGH)
    grad_c = jnp.einsum("gts,sgn->tgn", joint, basis_in, precision=HIGH)
    grad_c = grad_c + jnp.einsum("tgk,tgkn->tgn", leading, state_read, precision=HIGH)
    entry_term = leading * jnp.sum(state_read * basis_out[:, :, None, :], axis=-1)
    exit_term = tail * step_grid * jnp.sum(inputs * carried, axis=-1)
    closing = jnp.exp(final) * jnp.sum(later * entry, axis=(2, 3)) + jnp.sum(exit_term, axis=0)
    grad_cum = change + entry_term - exit_term
    grad_log = jnp.cumsum(grad_cum[::-1], axis=0)[::-1] + closing[None]
    grad_step = direct - rate_grid[None] * grad_log
    grad_raw = grad_step.reshape(length, heads) * jax.nn.sigmoid(raw)
    columns = tokens.astype(jnp.float32)
    partial_rows = lax.psum_scatter(
        jnp.dot(columns.T, grad_raw, precision=HIGH), "fsdp", scatter_dimension=0, tiled=True
    )
    grad_weight = lax.psum(partial_rows, "seq")
    out_x = grad_x.reshape(1, length, heads * head_size).astype(jnp.bfloat16)
    out_b = grad_b.reshape(1, length, groups * STATE).astype(jnp.bfloat16)
    out_c = grad_c.reshape(1, length, groups * STATE).astype(jnp.bfloat16)
    return (out_x, out_b, out_c, grad_weight)


def solution(mesh):
    placed = (
        P("fsdp", "seq", None),
        P("fsdp", None),
        P(),
        P(),
        P("fsdp", "seq", None),
        P("fsdp", "seq", None),
        P("fsdp", "seq", None),
        P("fsdp", "seq", None),
    )
    return jax.shard_map(
        body,
        mesh=mesh,
        in_specs=placed,
        out_specs=(
            P("fsdp", "seq", None),
            P("fsdp", "seq", None),
            P("fsdp", "seq", None),
            P("fsdp", None),
        ),
        check_vma=False,
    )
```

profile of v0, /device:TPU:0, one launch (start us, length us, event | category | flops | bytes accessed | tf_op | source)
XLA Modules:
  0.0 256.8 jit_solution(15940278393139724668)
XLA Ops:
  7.2 11.8 %all_gather.17 = bf16[4096,64]{0,1:T(8,128)(2,1)S(1)} all-gather(bf16[512,64]{0,1:T(8,128)(2,1)} %param.13), channel_id=1, replica_groups=mesh['fsdp'=8,'seq'=4] {'fsdp'}, dimensions={0}, use_global_device_ids=true | all-gather | bytes 589824 | tf_op jit(solution)/shard_map/all_gather | solution.py:68
  19.7 1.8 compare_select_fusion
  22.4 0.9 reshape_squeeze.13
  23.3 1.3 copy.82
  25.5 1.4 convolution_convert_fusion
  27.3 1.6 fusion.26
  30.1 11.6 %all-gather = f32[4,1,64]{2,1,0:T(1,128)S(1)} all-gather(f32[1,1,64]{2,1,0:T(1,128)} %get-tuple-element.277), channel_id=1, replica_groups=mesh['fsdp'=8,'seq'=4] {'seq'}, dimensions={0}, use_global_device_ids=true | all-gather | bytes 1280 | tf_op jit(solution)/shard_map/all_gather | solution.py:35
  42.4 8.4 %all-gather.1 = bf16[4,1,64]{2,1,0:T(2,128)(2,1)S(1)} all-gather(bf16[1,1,64]{2,1,0:T(2,128)(2,1)} %get-tuple-element.278), channel_id=1, replica_groups=mesh['fsdp'=8,'seq'=4] {'seq'}, dimensions={0}, use_global_device_ids=true | all-gather | bytes 640 | tf_op jit(solution)/shard_map/all_gather | solution.py:13
  53.1 5.1 %multiply_reduce_fusion = (f32[4,16,128]{2,1,0:T(8,128)}, f32[4,16,128]{2,1,0:T(8,128)}, f32[4,128,128]{2,1,0:T(8,128)}) fusion(f32[4,128,128]{2,1,0:T(8,128)S(1)} %fusion.40, f32[4,16,128]{2,1,0:T(8,128)} %bitcast.131, bf16[128,4,16,32]{0,3,2,1:T(8,128)(2,1)} %bitcast.120, bf16[128,4,16,32]{0,3,2,1:T(8,128)(2,1)} %bitcast.112, ...), kind=kOutput, calls=%fused_computation.15 | convolution fusion | flops 76464128 | bytes 1720320 | tf_op jit(solution)/shard_map/tgkp,sgkp->gkts/dot_general | solution.py:112
  58.2 14.8 %all-gather.7.cloned.1.call-done = bf16[4,64,32,128]{3,2,1,0:T(8,128)(2,1)} async-done(((bf16[1,64,32,128]{3,2,1,0:T(8,128)(2,1)}), bf16[4,64,32,128]{3,2,1,0:T(8,128)(2,1)}) %all-gather.7.cloned.1.call-update) | async-done | bytes 2097168 | tf_op jit(solution)/shard_map/all_gather | solution.py:13
  73.0 8.2 %while.29 = (s32[]{:T(128)}, f32[64,32,128]{2,1,0:T(8,128)S(1)}, s32[]{:T(128)}, bf16[4,64,32,128]{3,2,1,0:T(8,128)(2,1)}, bf16[4,64]{1,0:T(4,128)(2,1)}, /*index=5*/s32[]{:T(128)}, s32[]{:T(128)}) while((s32[]{:T(128)}, f32[64,32,128]{2,1,0:T(8,128)S(1)}, s32[]{:T(128)}, bf16[4,64,32,128]{3,2,1,0:T(8,128)(2,1)}, ...), condition=%wide.region_5.6_spmd.clone, body=%wide.region_4.5_spmd.clone.sunk | while | flops 1310788 | bytes 2622185 | solution.py:30
  73.7 1.4 fusion.60
  75.8 1.4 fusion.60
  77.8 1.4 fusion.60
  79.9 1.4 fusion.60
  81.3 5.4 %fusion.3 = (f32[128,4,16]{0,2,1:T(8,128)}, f32[128,4,128]{0,2,1:T(8,128)}) fusion(f32[128,4,128]{0,2,1:T(8,128)} %convert_element_type.107, f32[128,4,16]{0,2,1:T(8,128)} %copy-done.19, f32[4,16,32,128]{3,2,1,0:T(8,128)S(1)} %bitcast.110, bf16[128,4,16,32]{0,3,2,1:T(8,128)(2,1)} %bitcast.121), kind=kOutput, calls=%fused_computation.10 | convolution fusion | flops 406773760 | bytes 2162688 | tf_op jit(solution)/shard_map/tgkp,gkpn->tgkn/dot_general | solution.py:128
  86.6 67.5 %all-gather.5.cloned.1.call-done = f32[4,64,32,128]{3,2,1,0:T(8,128)} async-done(((f32[1,64,32,128]{3,2,1,0:T(8,128)}), f32[4,64,32,128]{3,2,1,0:T(8,128)}) %all-gather.5.cloned.1.call-update) | async-done | bytes 4194320 | tf_op jit(solution)/shard_map/all_gather | solution.py:35
  154.2 4.6 %rev.12 = f32[4,64,32,128]{3,2,1,0:T(8,128)} reverse(f32[4,64,32,128]{3,2,1,0:T(8,128)} %all-gather.5.cloned.1.call-done), dimensions={0} | reverse | bytes 8388608 | tf_op jit(solution)/shard_map/rev | solution.py:36
  158.8 6.6 %while.28 = (s32[]{:T(128)}, f32[64,32,128]{2,1,0:T(8,128)S(1)}, s32[]{:T(128)}, f32[4,64,32,128]{3,2,1,0:T(8,128)}, f32[4,64]{1,0:T(4,128)}, /*index=5*/s32[]{:T(128)}, s32[]{:T(128)}) while((s32[]{:T(128)}, f32[64,32,128]{2,1,0:T(8,128)S(1)}, s32[]{:T(128)}, f32[4,64,32,128]{3,2,1,0:T(8,128)}, f32[4,64]{1,0:T(4,128)}, ...), condition=%wide.region_2.3_spmd.clone, body=%wide.region_1.2_spmd.clone.sunk | while | flops 1048580 | bytes 3146601 | solution.py:46
  159.5 1.5 fusion.59
  161.6 1.5 fusion.59
  163.8 1.5 fusion.59
  165.4 1.1 multiply_reduce_fusion.2
  167.2 4.9 %fusion.23 = (f32[128,4,16]{0,2,1:T(8,128)S(1)}, f32[128,4,16]{0,2,1:T(8,128)}, bf16[128,4,16,32]{0,3,2,1:T(8,128)(2,1)}) fusion(f32[128,4,16,32]{0,3,2,1:T(8,128)S(1)} %convolution_bitcast_fusion.1, bf16[128,4,16,32]{0,3,2,1:T(8,128)(2,1)S(1)} %bitcast.113, f32[128,4,16]{0,2,1:T(8,128)S(1)} %bitcast.132, f32[128,4,16]{0,2,1:T(8,128)S(1)} %copy-done.23, ...), kind=kOutput, calls=%fused_computation.38 | convolution fusion | flops 409190400 | bytes 3063808 | tf_op jit(solution)/shard_map/gkts,tgkp->sgkp/dot_general | solution.py:115
  173.6 1.0 copy.88
  175.6 1.5 convolution_bitcast_fusion
  177.5 1.3 fusion.21
  179.6 1.8 fusion.18
  181.4 30.4 %reduce-scatter.2.cloned.1.call-done = f32[512,64]{0,1:T(8,128)} async-done(((f32[4096,64]{0,1:T(8,128)}), f32[512,64]{0,1:T(8,128)}) %reduce-scatter.2.cloned.1.call-update) | async-done | bytes 131088 | tf_op jit(solution)/shard_map/reduce_scatter | solution.py:139
  212.9 2.0 copy.90
  215.0 33.7 %all-reduce.2.cloned.1.call-done = f32[512,64]{0,1:T(8,128)} async-done(((f32[512,64]{0,1:T(8,128)}), f32[512,64]{0,1:T(8,128)}) %all-reduce.2.cloned.1.call-update) | async-done | bytes 131088 | tf_op jit(solution)/shard_map/psum | solution.py:142
  248.7 1.6 copy.131
  (103 shorter events, 16.8 us)
Async XLA Ops:
  7.2 12.5 %copy-start = (bf16[1,128,4096]{2,1,0:T(8,128)(2,1)S(1)}, bf16[1,128,4096]{2,1,0:T(8,128)(2,1)}, u32[]{:S(2)}) copy-start(bf16[1,128,4096]{2,1,0:T(8,128)(2,1)} %param.12) | copy-start | bytes 3145732
  7.2 19.8 %copy-start.12 = (bf16[1,128,2048]{2,1,0:T(8,128)(2,1)S(1)}, bf16[1,128,2048]{2,1,0:T(8,128)(2,1)}, u32[]{:S(2)}) copy-start(bf16[1,128,2048]{2,1,0:T(8,128)(2,1)} %param.19) | copy-start | bytes 1572868
  7.2 20.1 %copy-start.16 = (bf16[1,128,512]{2,1,0:T(8,128)(2,1)S(1)}, bf16[1,128,512]{2,1,0:T(8,128)(2,1)}, u32[]{:S(2)}) copy-start(bf16[1,128,512]{2,1,0:T(8,128)(2,1)} %param.18) | copy-start | bytes 393220
  7.2 65.8 %all-gather.7.cloned.1.call-start = ((), (), s32[]{:S(2)}) async-start(), calls=%async_computation.2 | async-start | bytes 2621440 | tf_op jit(solution)/shard_map/all_gather | solution.py:13
  21.4 5.5 %copy-start.17 = (f32[128,64]{0,1:T(8,128)}, f32[128,64]{0,1:T(8,128)S(1)}, u32[]{:S(2)}) copy-start(f32[128,64]{0,1:T(8,128)S(1)} %get-tuple-element.281) | copy-start | bytes 98308
  22.3 4.6 %copy-start.9 = (f32[128,64]{0,1:T(8,128)}, f32[128,64]{0,1:T(8,128)S(1)}, u32[]{:S(2)}) copy-start(f32[128,64]{0,1:T(8,128)S(1)} %copy.76) | copy-start | bytes 98308
  24.7 4.4 %copy-start.1 = (bf16[1,128,2048]{1,2,0:T(8,128)(2,1)}, bf16[1,128,2048]{1,2,0:T(8,128)(2,1)S(1)}, u32[]{:S(2)}) copy-start(bf16[1,128,2048]{1,2,0:T(8,128)(2,1)S(1)} %copy.82) | copy-start | bytes 1572868
  25.4 1.5 copy-start.7
  25.5 3.8 %copy-start.19 = (f32[128,4,16]{0,2,1:T(8,128)}, f32[128,4,16]{0,2,1:T(8,128)S(1)}, u32[]{:S(2)}) copy-start(f32[128,4,16]{0,2,1:T(8,128)S(1)} %get-tuple-element.280) | copy-start | bytes 98308
  26.9 127.2 %all-gather.5.cloned.1.call-start = ((), (), s32[]{:S(2)}) async-start(), calls=%async_computation.1 | async-start | bytes 5242880 | tf_op jit(solution)/shard_map/all_gather | solution.py:35
  27.3 1.8 copy-start.4
  29.0 182.9 %reduce-scatter.2.cloned.1.call-start = ((), (), s32[]{:S(2)}) async-start(), calls=%async_computation.3 | async-start | bytes 1179648 | tf_op jit(solution)/shard_map/reduce_scatter | solution.py:139
  52.1 0.6 copy-start.24
  52.3 0.7 copy-start.14
  165.3 1.8 copy-start.2
  165.3 1.8 copy-start.5
  165.4 1.8 copy-start.10
  165.4 1.8 copy-start.15
  165.4 1.8 copy-start.18
  165.4 1.8 copy-start.23
  165.4 1.8 copy-start.25
  167.2 5.0 %copy-start.13 = (f32[128,64]{0,1:T(8,128)S(1)}, f32[128,64]{0,1:T(8,128)}, u32[]{:S(2)}) copy-start(f32[128,64]{0,1:T(8,128)} %get-tuple-element.283) | copy-start | bytes 98308
  167.2 5.2 %copy-start.26 = (f32[64]{0:T(128)S(1)}, f32[64]{0:T(128)}, u32[]{:S(2)}) copy-start(f32[64]{0:T(128)} %multiply_reduce_fusion.2) | copy-start | bytes 772
  167.2 5.3 %copy-start.8 = (f32[128,4,16]{0,2,1:T(8,128)S(1)}, f32[128,4,16]{0,2,1:T(8,128)}, u32[]{:S(2)}) copy-start(f32[128,4,16]{0,2,1:T(8,128)} %copy-done.7) | copy-start | bytes 98308
  167.2 5.3 %copy-start.11 = (f32[128,64]{0,1:T(8,128)S(1)}, f32[128,64]{0,1:T(8,128)}, u32[]{:S(2)}) copy-start(f32[128,64]{0,1:T(8,128)} %copy-done.9) | copy-start | bytes 98308
  167.2 5.3 %copy-start.20 = (f32[4,16,128]{2,1,0:T(8,128)S(1)}, f32[4,16,128]{2,1,0:T(8,128)}, u32[]{:S(2)}) copy-start(f32[4,16,128]{2,1,0:T(8,128)} %get-tuple-element.246) | copy-start | bytes 98308
  167.2 5.3 %copy-start.21 = (f32[4,16,128]{2,1,0:T(8,128)S(1)}, f32[4,16,128]{2,1,0:T(8,128)}, u32[]{:S(2)}) copy-start(f32[4,16,128]{2,1,0:T(8,128)} %get-tuple-element.247) | copy-start | bytes 98308
  167.2 5.3 %copy-start.22 = (f32[128,4,16]{0,2,1:T(8,128)S(1)}, f32[128,4,16]{0,2,1:T(8,128)}, u32[]{:S(2)}) copy-start(f32[128,4,16]{0,2,1:T(8,128)} %get-tuple-element.249) | copy-start | bytes 98308
  172.1 5.4 %copy-start.6 = (f32[4,128,128]{2,1,0:T(8,128)S(1)}, f32[4,128,128]{2,1,0:T(8,128)}, u32[]{:S(2)}) copy-start(f32[4,128,128]{2,1,0:T(8,128)} %get-tuple-element.248) | copy-start | bytes 786436
  172.1 7.5 %copy-start.3 = (bf16[1,128,2048]{1,2,0:T(8,128)(2,1)S(1)}, bf16[1,128,2048]{1,2,0:T(8,128)(2,1)}, u32[]{:S(2)}) copy-start(bf16[1,128,2048]{1,2,0:T(8,128)(2,1)} %copy-done.1) | copy-start | bytes 1572868
  177.2 71.5 %all-reduce.2.cloned.1.call-start = ((), (), s32[]{:S(2)}) async-start(), calls=%async_computation.4 | async-start | bytes 262144 | tf_op jit(solution)/shard_map/psum | solution.py:142
Sparse Core Ops, SparseCore 0:
  27.0 45.9 all-gather.6
  74.6 79.5 all-gather.4
  177.3 34.4 reduce-scatter.1
  214.0 34.6 all-reduce.1
where the time goes:
time: 258 us; the launch traced here: 257 us
  waiting for transfers between devices  147 us (57%)
  blocking collectives  31.8 us (12%)
  matrix products  26 us (10%)
  local copies, waits for them, and re-layouts  19.2 us (7%)
  other arithmetic  18.5 us (7%)
  between operations  14.3 us (6%)
    all_gather x1, waiting for transfers between devices, prefix(): pieces = jax.tree.map(lambda part: lax.all_gather(part, axis), value)  67.5 us
    psum x1, waiting for transfers between devices, body(): grad_weight = lax.psum(partial_rows, 'seq')  33.7 us
    reduce_scatter x1, waiting for transfers between devices, body(): lax.psum_scatter(jnp.dot(columns.T, grad_raw, precision=HIGH), 'fsdp', sc...  30.4 us
    all_gather x1, waiting for transfers between devices, entering(): lax.all_gather(part.astype(kind), axis)  14.8 us
    all_gather x1, blocking collectives, body(): lax.all_gather(dt_weight, 'fsdp', axis=0, tiled=True)  11.8 us
    all_gather x1, blocking collectives, prefix(): pieces = jax.tree.map(lambda part: lax.all_gather(part, axis), value)  11.6 us
    all_gather x1, blocking collectives, entering(): lax.all_gather(part.astype(kind), axis)  8.39 us
    unnamed x61, local copies, waits for them, and re-layouts  8.16 us
  transfers between devices with their start and end apart: 4, of which 4 were waited for; matrix products, arithmetic and copies ran while one was open for 12% of the time, Pallas kernels for 0%

commit v1 on v0

--- a/solution.py
+++ b/solution.py
@@ -139,7 +139,7 @@
     partial_rows = lax.psum_scatter(
         jnp.dot(columns.T, grad_raw, precision=HIGH), "fsdp", scatter_dimension=0, tiled=True
     )
-    grad_weight = lax.psum(partial_rows, "seq")
+    grad_weight = jnp.sum(lax.all_gather(partial_rows, "seq"), axis=0)
     out_x = grad_x.reshape(1, length, heads * head_size).astype(jnp.bfloat16)
     out_b = grad_b.reshape(1, length, groups * STATE).astype(jnp.bfloat16)
     out_c = grad_c.reshape(1, length, groups * STATE).astype(jnp.bfloat16)

time: 258 us -> 238 us (0.922)
  waiting for transfers between devices: 147 us -> 111 us
  blocking collectives: 31.8 us -> 46.9 us
    psum x1 -> x0, waiting for transfers between devices: 33.7 us -> none  [body(): grad_weight = lax.psum(partial_rows, 'seq')]
    all_gather x0 -> x1, blocking collectives: none -> 15.6 us  [body(): grad_weight = jnp.sum(lax.all_gather(partial_rows, 'seq'), axis=0)]
    reduce_scatter x1, waiting for transfers between devices: 30.4 us -> 27.6 us  [body(): lax.psum_scatter(jnp.dot(columns.T, grad_raw, precision=HIGH), 'fsdp', sc...]
    unnamed x61 -> x52, local copies, waits for them, and re-layouts: 8.16 us -> 6.55 us
  transfers between devices with their start and end apart: 4 -> 3, of which waited for: 4 -> 3; matrix products, arithmetic and copies ran while one was open for 12% -> 13% of each run, Pallas kernels for 0% -> 0%
where the time goes in v1:
time: 238 us; the launch traced here: 237 us
  waiting for transfers between devices  111 us (47%)
  blocking collectives  46.9 us (20%)
  matrix products  26.1 us (11%)
  other arithmetic  20.2 us (8%)
  local copies, waits for them, and re-layouts  18.6 us (8%)
  between operations  14.2 us (6%)
    all_gather x1, waiting for transfers between devices, prefix(): pieces = jax.tree.map(lambda part: lax.all_gather(part, axis), value)  67.7 us
    reduce_scatter x1, waiting for transfers between devices, body(): lax.psum_scatter(jnp.dot(columns.T, grad_raw, precision=HIGH), 'fsdp', sc...  27.6 us
    all_gather x1, blocking collectives, body(): grad_weight = jnp.sum(lax.all_gather(partial_rows, 'seq'), axis=0)  15.6 us
    all_gather x1, waiting for transfers between devices, entering(): lax.all_gather(part.astype(kind), axis)  15.4 us
    all_gather x1, blocking collectives, body(): lax.all_gather(dt_weight, 'fsdp', axis=0, tiled=True)  11.8 us
    all_gather x1, blocking collectives, prefix(): pieces = jax.tree.map(lambda part: lax.all_gather(part, axis), value)  11.4 us
    all_gather x1, blocking collectives, entering(): lax.all_gather(part.astype(kind), axis)  8.06 us
    unnamed x52, local copies, waits for them, and re-layouts  6.55 us
  transfers between devices with their start and end apart: 3, of which 3 were waited for; matrix products, arithmetic and copies ran while one was open for 13% of the time, Pallas kernels for 0%

profile of v1, /device:TPU:0, one launch (start us, length us, event | category | flops | bytes accessed | tf_op | source)
XLA Modules:
  0.0 236.8 jit_solution(5984092048151173802)
XLA Ops:
  7.2 11.8 %all_gather.23 = bf16[4096,64]{0,1:T(8,128)(2,1)S(1)} all-gather(bf16[512,64]{0,1:T(8,128)(2,1)} %param.13), channel_id=1, replica_groups=mesh['fsdp'=8,'seq'=4] {'fsdp'}, dimensions={0}, use_global_device_ids=true | all-gather | bytes 589824 | tf_op jit(solution)/shard_map/all_gather | solution.py:68
  19.7 1.8 compare_select_fusion
  22.5 0.9 reshape_squeeze.13
  23.4 1.3 copy.82
  25.5 1.4 convolution_convert_fusion
  27.4 1.7 fusion.26
  30.2 11.4 %all-gather.1 = f32[4,1,64]{2,1,0:T(1,128)S(1)} all-gather(f32[1,1,64]{2,1,0:T(1,128)} %get-tuple-element.277), channel_id=1, replica_groups=mesh['fsdp'=8,'seq'=4] {'seq'}, dimensions={0}, use_global_device_ids=true | all-gather | bytes 1280 | tf_op jit(solution)/shard_map/all_gather | solution.py:35
  42.3 8.1 %all-gather.2 = bf16[4,1,64]{2,1,0:T(2,128)(2,1)S(1)} all-gather(bf16[1,1,64]{2,1,0:T(2,128)(2,1)} %get-tuple-element.278), channel_id=1, replica_groups=mesh['fsdp'=8,'seq'=4] {'seq'}, dimensions={0}, use_global_device_ids=true | all-gather | bytes 640 | tf_op jit(solution)/shard_map/all_gather | solution.py:13
  52.6 5.1 %multiply_reduce_fusion = (f32[4,16,128]{2,1,0:T(8,128)}, f32[4,16,128]{2,1,0:T(8,128)}, f32[4,128,128]{2,1,0:T(8,128)}) fusion(f32[4,128,128]{2,1,0:T(8,128)S(1)} %fusion.40, f32[4,16,128]{2,1,0:T(8,128)} %bitcast.133, bf16[128,4,16,32]{0,3,2,1:T(8,128)(2,1)} %bitcast.122, bf16[128,4,16,32]{0,3,2,1:T(8,128)(2,1)} %bitcast.114, ...), kind=kOutput, calls=%fused_computation.15 | convolution fusion | flops 76464128 | bytes 1720320 | tf_op jit(solution)/shard_map/tgkp,sgkp->gkts/dot_general | solution.py:112
  57.7 15.4 %all-gather.8.cloned.1.call-done = bf16[4,64,32,128]{3,2,1,0:T(8,128)(2,1)} async-done(((bf16[1,64,32,128]{3,2,1,0:T(8,128)(2,1)}), bf16[4,64,32,128]{3,2,1,0:T(8,128)(2,1)}) %all-gather.8.cloned.1.call-update) | async-done | bytes 2097168 | tf_op jit(solution)/shard_map/all_gather | solution.py:13
  73.1 8.0 %while.29 = (s32[]{:T(128)}, f32[64,32,128]{2,1,0:T(8,128)S(1)}, s32[]{:T(128)}, bf16[4,64,32,128]{3,2,1,0:T(8,128)(2,1)}, bf16[4,64]{1,0:T(4,128)(2,1)}, /*index=5*/s32[]{:T(128)}, s32[]{:T(128)}) while((s32[]{:T(128)}, f32[64,32,128]{2,1,0:T(8,128)S(1)}, s32[]{:T(128)}, bf16[4,64,32,128]{3,2,1,0:T(8,128)(2,1)}, ...), condition=%wide.region_5.6_spmd.clone, body=%wide.region_4.5_spmd.clone.sunk | while | flops 1310788 | bytes 2622185 | solution.py:30
  73.7 1.4 fusion.60
  75.7 1.4 fusion.60
  77.7 1.4 fusion.60
  79.7 1.4 fusion.60
  81.2 5.4 %fusion.3 = (f32[128,4,16]{0,2,1:T(8,128)}, f32[128,4,128]{0,2,1:T(8,128)}) fusion(f32[128,4,128]{0,2,1:T(8,128)} %convert_element_type.107, f32[128,4,16]{0,2,1:T(8,128)} %copy-done.19, f32[4,16,32,128]{3,2,1,0:T(8,128)S(1)} %bitcast.112, bf16[128,4,16,32]{0,3,2,1:T(8,128)(2,1)} %bitcast.123), kind=kOutput, calls=%fused_computation.10 | convolution fusion | flops 406773760 | bytes 2162688 | tf_op jit(solution)/shard_map/tgkp,gkpn->tgkn/dot_general | solution.py:128
  86.6 67.7 %all-gather.6.cloned.1.call-done = f32[4,64,32,128]{3,2,1,0:T(8,128)} async-done(((f32[1,64,32,128]{3,2,1,0:T(8,128)}), f32[4,64,32,128]{3,2,1,0:T(8,128)}) %all-gather.6.cloned.1.call-update) | async-done | bytes 4194320 | tf_op jit(solution)/shard_map/all_gather | solution.py:35
  154.3 4.6 %rev.12 = f32[4,64,32,128]{3,2,1,0:T(8,128)} reverse(f32[4,64,32,128]{3,2,1,0:T(8,128)} %all-gather.6.cloned.1.call-done), dimensions={0} | reverse | bytes 8388608 | tf_op jit(solution)/shard_map/rev | solution.py:36
  158.8 6.5 %while.28 = (s32[]{:T(128)}, f32[64,32,128]{2,1,0:T(8,128)S(1)}, s32[]{:T(128)}, f32[4,64,32,128]{3,2,1,0:T(8,128)}, f32[4,64]{1,0:T(4,128)}, /*index=5*/s32[]{:T(128)}, s32[]{:T(128)}) while((s32[]{:T(128)}, f32[64,32,128]{2,1,0:T(8,128)S(1)}, s32[]{:T(128)}, f32[4,64,32,128]{3,2,1,0:T(8,128)}, f32[4,64]{1,0:T(4,128)}, ...), condition=%wide.region_2.3_spmd.clone, body=%wide.region_1.2_spmd.clone.sunk | while | flops 1048580 | bytes 3146601 | solution.py:46
  159.5 1.5 fusion.59
  161.7 1.5 fusion.59
  163.9 1.5 fusion.59
  165.5 1.1 multiply_reduce_fusion.2
  167.3 4.9 %fusion.23 = (f32[128,4,16]{0,2,1:T(8,128)S(1)}, f32[128,4,16]{0,2,1:T(8,128)}, bf16[128,4,16,32]{0,3,2,1:T(8,128)(2,1)}) fusion(f32[128,4,16,32]{0,3,2,1:T(8,128)S(1)} %convolution_bitcast_fusion.1, bf16[128,4,16,32]{0,3,2,1:T(8,128)(2,1)S(1)} %bitcast.115, f32[128,4,16]{0,2,1:T(8,128)S(1)} %bitcast.134, f32[128,4,16]{0,2,1:T(8,128)S(1)} %copy-done.20, ...), kind=kOutput, calls=%fused_computation.38 | convolution fusion | flops 409190400 | bytes 3063808 | tf_op jit(solution)/shard_map/gkts,tgkp->sgkp/dot_general | solution.py:115
  175.2 1.0 copy.88
  177.2 1.6 convolution_bitcast_fusion
  178.8 1.3 fusion.21
  180.9 1.8 fusion.18
  183.8 2.1 copy.90
  185.8 27.6 %reduce-scatter.2.cloned.1.call-done = f32[512,64]{0,1:T(8,128)} async-done(((f32[4096,64]{0,1:T(8,128)}), f32[512,64]{0,1:T(8,128)}) %reduce-scatter.2.cloned.1.call-update) | async-done | bytes 131088 | tf_op jit(solution)/shard_map/reduce_scatter | solution.py:139
  213.4 15.6 %all-gather = f32[2048,64]{0,1:T(8,128)S(1)} all-gather(f32[512,64]{0,1:T(8,128)} %reduce-scatter.2.cloned.1.call-done), channel_id=2, replica_groups=mesh['fsdp'=8,'seq'=4] {'seq'}, dimensions={0}, use_global_device_ids=true | all-gather | bytes 655360 | tf_op jit(solution)/shard_map/all_gather | solution.py:142
  229.3 1.0 reduce_sum.98
  (94 shorter events, 18.1 us)
Async XLA Ops:
  7.2 12.5 %copy-start = (bf16[1,128,4096]{2,1,0:T(8,128)(2,1)S(1)}, bf16[1,128,4096]{2,1,0:T(8,128)(2,1)}, u32[]{:S(2)}) copy-start(bf16[1,128,4096]{2,1,0:T(8,128)(2,1)} %param.12) | copy-start | bytes 3145732
  7.2 19.9 %copy-start.12 = (bf16[1,128,2048]{2,1,0:T(8,128)(2,1)S(1)}, bf16[1,128,2048]{2,1,0:T(8,128)(2,1)}, u32[]{:S(2)}) copy-start(bf16[1,128,2048]{2,1,0:T(8,128)(2,1)} %param.19) | copy-start | bytes 1572868
  7.2 20.2 %copy-start.16 = (bf16[1,128,512]{2,1,0:T(8,128)(2,1)S(1)}, bf16[1,128,512]{2,1,0:T(8,128)(2,1)}, u32[]{:S(2)}) copy-start(bf16[1,128,512]{2,1,0:T(8,128)(2,1)} %param.18) | copy-start | bytes 393220
  7.2 65.9 %all-gather.8.cloned.1.call-start = ((), (), s32[]{:S(2)}) async-start(), calls=%async_computation.2 | async-start | bytes 2621440 | tf_op jit(solution)/shard_map/all_gather | solution.py:13
  21.4 5.6 %copy-start.17 = (f32[128,64]{0,1:T(8,128)}, f32[128,64]{0,1:T(8,128)S(1)}, u32[]{:S(2)}) copy-start(f32[128,64]{0,1:T(8,128)S(1)} %get-tuple-element.281) | copy-start | bytes 98308
  22.4 4.6 %copy-start.9 = (f32[128,64]{0,1:T(8,128)}, f32[128,64]{0,1:T(8,128)S(1)}, u32[]{:S(2)}) copy-start(f32[128,64]{0,1:T(8,128)S(1)} %copy.76) | copy-start | bytes 98308
  24.7 4.4 %copy-start.1 = (bf16[1,128,2048]{1,2,0:T(8,128)(2,1)}, bf16[1,128,2048]{1,2,0:T(8,128)(2,1)S(1)}, u32[]{:S(2)}) copy-start(bf16[1,128,2048]{1,2,0:T(8,128)(2,1)S(1)} %copy.82) | copy-start | bytes 1572868
  25.5 1.5 copy-start.7
  25.5 3.8 %copy-start.19 = (f32[128,4,16]{0,2,1:T(8,128)}, f32[128,4,16]{0,2,1:T(8,128)S(1)}, u32[]{:S(2)}) copy-start(f32[128,4,16]{0,2,1:T(8,128)S(1)} %get-tuple-element.280) | copy-start | bytes 98308
  27.0 127.2 %all-gather.6.cloned.1.call-start = ((), (), s32[]{:S(2)}) async-start(), calls=%async_computation.1 | async-start | bytes 5242880 | tf_op jit(solution)/shard_map/all_gather | solution.py:35
  27.4 1.8 copy-start.4
  29.1 184.3 %reduce-scatter.2.cloned.1.call-start = ((), (), s32[]{:S(2)}) async-start(), calls=%async_computation.3 | async-start | bytes 1179648 | tf_op jit(solution)/shard_map/reduce_scatter | solution.py:139
  51.6 0.6 copy-start.21
  51.9 0.7 copy-start.14
  165.4 1.8 copy-start.2
  165.4 1.8 copy-start.5
  165.4 1.8 copy-start.10
  165.4 1.8 copy-start.15
  165.4 1.8 copy-start.18
  165.4 1.8 copy-start.20
  165.5 1.8 copy-start.22
  167.3 4.9 %copy-start.13 = (f32[128,64]{0,1:T(8,128)S(1)}, f32[128,64]{0,1:T(8,128)}, u32[]{:S(2)}) copy-start(f32[128,64]{0,1:T(8,128)} %get-tuple-element.283) | copy-start | bytes 98308
  167.3 5.9 %copy-start.8 = (f32[128,4,16]{0,2,1:T(8,128)S(1)}, f32[128,4,16]{0,2,1:T(8,128)}, u32[]{:S(2)}) copy-start(f32[128,4,16]{0,2,1:T(8,128)} %copy-done.7) | copy-start | bytes 98308
  167.3 5.9 %copy-start.11 = (f32[128,64]{0,1:T(8,128)S(1)}, f32[128,64]{0,1:T(8,128)}, u32[]{:S(2)}) copy-start(f32[128,64]{0,1:T(8,128)} %copy-done.9) | copy-start | bytes 98308
  172.2 6.6 %copy-start.6 = (f32[4,128,128]{2,1,0:T(8,128)S(1)}, f32[4,128,128]{2,1,0:T(8,128)}, u32[]{:S(2)}) copy-start(f32[4,128,128]{2,1,0:T(8,128)} %get-tuple-element.248) | copy-start | bytes 786436
  172.2 8.7 %copy-start.3 = (bf16[1,128,2048]{1,2,0:T(8,128)(2,1)S(1)}, bf16[1,128,2048]{1,2,0:T(8,128)(2,1)}, u32[]{:S(2)}) copy-start(bf16[1,128,2048]{1,2,0:T(8,128)(2,1)} %copy-done.1) | copy-start | bytes 1572868
Sparse Core Ops, SparseCore 0:
  27.1 45.9 all-gather.7
  74.7 79.5 all-gather.5
  178.9 34.4 reduce-scatter.1
